TPU v7x, 32 devices: a whole 2x2x4 slice. The times are simulated.
32 devices in a mesh: dp: 4 (over x, core), fsdp: 8 (over z, y).
Axes of the slice: x: 2, y: 2, z: 4, core: 2. Of those that a mesh axis runs over, the one named last changes fastest.
Arguments:
- tokens: bfloat16 [32768, 768], P(('dp', 'fsdp')), may hold values from -6 to 6
- segment_ids: int32 [32768], P(('dp', 'fsdp')), may hold values from 0 to 543, as said below
- live_mask: int32 [32768], P(('dp', 'fsdp')), may hold values from 0 to 1, as said below
- cotangent: bfloat16 [32768, 768], P(('dp', 'fsdp')), may hold values from -6 to 6
- first_gain: bfloat16 [768], P(('dp', 'fsdp')), may hold values from 0.099609375 to 1.8984375
- first_shift: bfloat16 [768], P(('dp', 'fsdp')), may hold values from -4 to 4
- qkv_weight: bfloat16 [768, 2304], P(('dp', 'fsdp')), may hold values from -0.21875 to 0.21875
- query_bias: bfloat16 [768], P(('dp', 'fsdp')), may hold values from -4 to 4
- value_bias: bfloat16 [768], P(('dp', 'fsdp')), may hold values from -4 to 4
- proj_weight: bfloat16 [768, 768], P(('dp', 'fsdp')), may hold values from -1.75 to 1.75
- proj_bias: bfloat16 [768], P(('dp', 'fsdp')), may hold values from -4 to 4
- second_gain: bfloat16 [768], P(('dp', 'fsdp')), may hold values from 0.099609375 to 1.8984375
- second_shift: bfloat16 [768], P(('dp', 'fsdp')), may hold values from -4 to 4
- inner_weight: bfloat16 [768, 3072], P(('dp', 'fsdp')), may hold values from -0.21875 to 0.21875
- inner_bias: bfloat16 [3072], P(('dp', 'fsdp')), may hold values from -4 to 4
- outer_weight: bfloat16 [3072, 768], P(('dp', 'fsdp')), may hold values from -0.21875 to 0.21875
- outer_bias: bfloat16 [768], P(('dp', 'fsdp')), may hold values from -4 to 4
Outputs:
- layer_out: bfloat16 [32768, 768], P(('dp', 'fsdp'))
- grad_tokens: bfloat16 [32768, 768], P(('dp', 'fsdp'))
- grad_first_gain: float32 [768], P(('dp', 'fsdp'))
- grad_first_shift: float32 [768], P(('dp', 'fsdp'))
- grad_qkv: float32 [768, 2304], P(('dp', 'fsdp'))
- grad_query_bias: float32 [768], P(('dp', 'fsdp'))
- grad_value_bias: float32 [768], P(('dp', 'fsdp'))
- grad_proj: float32 [768, 768], P(('dp', 'fsdp'))
- grad_proj_bias: float32 [768], P(('dp', 'fsdp'))
- grad_second_gain: float32 [768], P(('dp', 'fsdp'))
- grad_second_shift: float32 [768], P(('dp', 'fsdp'))
- grad_inner: float32 [768, 3072], P(('dp', 'fsdp'))
- grad_inner_bias: float32 [3072], P(('dp', 'fsdp'))
- grad_outer: float32 [3072, 768], P(('dp', 'fsdp'))
- grad_outer_bias: float32 [768], P(('dp', 'fsdp'))
Inputs may be any that keep to these rules, and one draw needn't show every extreme that they name: `segment_ids`: each aligned block of 1024 rows (the rows of one device) holds whole examples, each a run of consecutive rows with an id that no other example or block uses: image-text examples of 228 rows and text examples of 64 rows, in any order and number; the block's remaining rows at its end, 64 or more of them, share one further id of their own. `live_mask`: in an image-text example its 196 patch rows and its first 1 to 32 text rows are 1, in a text example its first 1 to 64 rows; all other rows are 0.
All inputs are finite; a program needn't handle non-finite values.
Results may differ from a plain program's by a relative error of at most 0.012.
Values may be sent and summed in bfloat16 or wider, within the bound.
A program may use at most 256 MiB of HBM per device.

v0:
```python
import jax
import jax.numpy as jnp
from jax import lax
from jax.experimental import pallas as pl
from jax.experimental.pallas import tpu as pltpu
from jax.sharding import PartitionSpec as P

D = 768
HEADS = 12
HEAD = 64
F32 = jnp.float32
BF16 = jnp.bfloat16
MESH = pl.DeviceIdType.MESH
AXES = ("dp", "fsdp")
epsilon = 1e-06
tanh_scale = 0.7978845608028654


def place():
    dp, fs = lax.axis_index("dp"), lax.axis_index("fsdp")
    return dp // 2, dp % 2, fs // 2, fs % 2

def device(x, c, z, y):
    return (x * 2 + c, z * 2 + y)

def peers(at):
    x, c, z, y = at
    return [device(x, c, (z + 1) % 4, y), device(x, c, (z + 2) % 4, y), device(x, c, (z + 3) % 4, y),
            device(x, c, z, 1 - y), device(1 - x, c, z, y), device(x, 1 - c, z, y)]

def greet(at):
    barrier = pltpu.get_barrier_semaphore()
    for peer in peers(at):
        pl.semaphore_signal(barrier, inc=1, device_id=peer, device_id_type=MESH)
    pl.semaphore_wait(barrier, 6)

def remote(src, dst, send, recv, to):
    return pltpu.make_async_remote_copy(src_ref=src, dst_ref=dst, send_sem=send, recv_sem=recv, device_id=to, device_id_type=MESH)

class Gather:
    def __init__(self, unit, at, src, out, cols, y_first, send, recv, local):
        x, c, z, y = at
        rows = src.shape[0]
        part = lambda yy: pl.ds(pl.multiple_of(yy * rows, 8), rows)
        s = lambda i: (send.at[unit, i], recv.at[unit, i])
        own = out.at[x, c, z, part(y), cols]
        self.keep = pltpu.make_async_copy(src.at[:, cols], own, local.at[unit])
        self.z = [remote(src.at[:, cols], own, *s(d), device(x, c, (z + d + 1) % 4, y)) for d in range(3)]
        line = out.at[x, c, :, part(y), cols]
        core = device(x, 1 - c, z, y)
        ydev, xdev = device(x, c, z, 1 - y), device(1 - x, c, z, y)
        if y_first:
            first, second = ydev, xdev
            got1 = out.at[x, c, :, part(1 - y), cols]
            held = out.at[x, c, :, :, cols]
            got2 = out.at[1 - x, c, :, :, cols]
        else:
            first, second = xdev, ydev
            got1 = out.at[1 - x, c, :, part(y), cols]
            held = out.at[:, c, :, part(y), cols]
            got2 = out.at[:, c, :, part(1 - y), cols]
        self.one = remote(line, line, *s(3), first)
        self.two = remote(held, held, *s(4), second)
        self.core = [remote(line, line, *s(5), core), remote(got1, got1, *s(6), core), remote(got2, got2, *s(7), core)]
    def start(self):
        self.keep.start()
        for copy in self.z:
            copy.start()
    def step1(self):
        self.keep.wait()
        for copy in self.z:
            copy.wait_recv()
        self.one.start()
        self.core[0].start()
    def step2(self):
        self.one.wait_recv()
        self.two.start()
        self.core[1].start()
    def step3(self):
        self.two.wait_recv()
        self.core[2].start()
    def arrive(self):
        for copy in self.core:
            copy.wait_recv()
    def sent(self):
        for copy in self.z + [self.one, self.two] + self.core:
            copy.wait_send()

BQ = 128
REACH = 2
NEG = -1e30

def window(block, blocks):
    return max(0, block - REACH), min(blocks, block + REACH + 1)

def nn(a, b):
    return lax.dot_general(a, b, (((1,), (0,)), ((), ())), preferred_element_type=F32)

def fill_bias(seg_row, key_code, bias_ref, blocks):
    slot = 0
    for b in range(blocks):
        low, high = window(b, blocks)
        q = seg_row[:, b * BQ:(b + 1) * BQ]
        for kb in range(low, high):
            code = key_code[kb * BQ:(kb + 1) * BQ, :]
            ok = code == q
            if kb == b:
                ok = ok | (lax.broadcasted_iota(jnp.int32, (BQ, BQ), 0) == lax.broadcasted_iota(jnp.int32, (BQ, BQ), 1))
            bias_ref[slot * BQ:(slot + 1) * BQ, :] = jnp.where(ok, 0.0, NEG)
            slot += 1

def slots_before(b, blocks):
    return sum(window(i, blocks)[1] - window(i, blocks)[0] for i in range(b))

def beside(top, low_rows):
    zero = jnp.zeros_like(top)
    return jnp.concatenate([jnp.where(low_rows, top, zero), jnp.where(low_rows, zero, top)], axis=1)

def fwd_kernel(seg_ref, code_ref, q_ref, k_ref, v_ref, o_ref, lse_ref, bias_ref):
    rows = q_ref.shape[0]
    blocks = rows // BQ
    @pl.when(pl.program_id(0) == 0)
    def _():
        fill_bias(seg_ref[...], code_ref[...], bias_ref, blocks)
    low_rows = lax.broadcasted_iota(jnp.int32, (2 * HEAD, BQ), 0) < HEAD
    vt = v_ref[...].T
    for b in range(blocks):
        low, high = window(b, blocks)
        at = slots_before(b, blocks)
        n = high - low
        qt = (q_ref[b * BQ:(b + 1) * BQ, :] * HEAD ** -0.5).T
        s = nn(k_ref[low * BQ:high * BQ, :], beside(qt, low_rows))
        bias = bias_ref[at * BQ:(at + n) * BQ, :]
        outs = []
        for h in range(2):
            sh = s[:, h * BQ:(h + 1) * BQ] + bias
            peak = jnp.max(sh, axis=0, keepdims=True)
            e = jnp.exp(sh - peak)
            total = jnp.sum(e, axis=0, keepdims=True)
            lse_ref[0, b:b + 1, h * BQ:(h + 1) * BQ] = peak + jnp.log(total)
            outs.append((e.astype(BF16), total))
        ot = nn(vt[:, low * BQ:high * BQ], jnp.concatenate([outs[0][0], outs[1][0]], axis=1))
        ot = jnp.concatenate([ot[:HEAD, :BQ] / outs[0][1], ot[HEAD:, BQ:] / outs[1][1]], axis=0)
        o_ref[b * BQ:(b + 1) * BQ, :] = ot.T.astype(BF16)

def bwd_kernel(seg_ref, code_ref, q_ref, k_ref, v_ref, o_ref, do_ref, lse_ref, dq_ref, dk_ref, dv_ref, bias_ref, dk_acc, dv_acc):
    rows = q_ref.shape[0]
    blocks = rows // BQ
    @pl.when(pl.program_id(0) == 0)
    def _():
        fill_bias(seg_ref[...], code_ref[...], bias_ref, blocks)
    low_rows = lax.broadcasted_iota(jnp.int32, (2 * HEAD, BQ), 0) < HEAD
    low_cols = lax.broadcasted_iota(jnp.int32, (BQ, 2 * HEAD), 1) < HEAD
    kt = k_ref[...].T
    dk_acc[...] = jnp.zeros_like(dk_acc)
    dv_acc[...] = jnp.zeros_like(dv_acc)
    def stack(x):
        zero = jnp.zeros_like(x)
        return jnp.concatenate([jnp.where(low_cols, x, zero), jnp.where(low_cols, zero, x)], axis=0)
    for b in range(blocks):
        low, high = window(b, blocks)
        at = slots_before(b, blocks)
        n = high - low
        here = slice(b * BQ, (b + 1) * BQ)
        q = q_ref[here, :] * HEAD ** -0.5
        do = do_ref[here, :]
        dprod = (do.astype(F32) * o_ref[here, :].astype(F32)).T
        keys = slice(low * BQ, high * BQ)
        s = nn(k_ref[keys, :], beside(q.T, low_rows))
        dp = nn(v_ref[keys, :], beside(do.T, low_rows))
        bias = bias_ref[at * BQ:(at + n) * BQ, :]
        ps, ds = [], []
        for h in range(2):
            cols = slice(h * BQ, (h + 1) * BQ)
            p = jnp.exp(s[:, cols] + bias - lse_ref[0, b:b + 1, cols])
            delta = jnp.sum(dprod[h * HEAD:(h + 1) * HEAD], axis=0, keepdims=True)
            ds.append((p * (dp[:, cols] - delta)).astype(BF16))
            ps.append(p.astype(BF16))
        p2 = jnp.concatenate(ps, axis=1)
        ds2 = jnp.concatenate(ds, axis=1)
        dv_acc[keys, :] += nn(p2, stack(do))
        dk_acc[keys, :] += nn(ds2, stack(q))
        dqt = nn(kt[:, keys], ds2)
        dqt = jnp.concatenate([dqt[:HEAD, :BQ], dqt[HEAD:, BQ:]], axis=0) * HEAD ** -0.5
        dq_ref[here, :] = dqt.T.astype(BF16)
    dk_ref[...] = dk_acc[...].astype(BF16)
    dv_ref[...] = dv_acc[...].astype(BF16)

def specs(rows):
    col = lambda off: pl.BlockSpec((rows, 2 * HEAD), lambda p: (0, p + off))
    full = lambda s: pl.BlockSpec(s, lambda p: (0,) * len(s))
    return col, full

def attn_fwd(seg_row, code_col, mixed):
    rows = mixed.shape[0]; width = mixed.shape[1] // 3; pairs = width // (2 * HEAD); blocks = rows // BQ
    col, full = specs(rows)
    return pl.pallas_call(fwd_kernel, grid=(pairs,),
        in_specs=[full((1, rows)), full((rows, 1)), col(0), col(pairs), col(2 * pairs)],
        out_specs=[col(0), pl.BlockSpec((1, blocks, 2 * BQ), lambda p: (p, 0, 0))],
        out_shape=[jax.ShapeDtypeStruct((rows, width), BF16), jax.ShapeDtypeStruct((pairs, blocks, 2 * BQ), F32)],
        scratch_shapes=[pltpu.VMEM((slots_before(blocks, blocks) * BQ, BQ), F32)],
        compiler_params=pltpu.CompilerParams(vmem_limit_bytes=60 * 2**20),
        )(seg_row, code_col, mixed, mixed, mixed)

def attn_bwd(seg_row, code_col, mixed, o, do, lse):
    rows = mixed.shape[0]; width = mixed.shape[1] // 3; pairs = width // (2 * HEAD); blocks = rows // BQ
    col, full = specs(rows)
    return pl.pallas_call(bwd_kernel, grid=(pairs,),
        in_specs=[full((1, rows)), full((rows, 1)), col(0), col(pairs), col(2 * pairs), col(0), col(0), pl.BlockSpec((1, blocks, 2 * BQ), lambda p: (p, 0, 0))],
        out_specs=[col(0), col(0), col(0)],
        out_shape=[jax.ShapeDtypeStruct((rows, width), BF16)] * 3,
        scratch_shapes=[pltpu.VMEM((slots_before(blocks, blocks) * BQ, BQ), F32), pltpu.VMEM((rows, 2 * HEAD), F32), pltpu.VMEM((rows, 2 * HEAD), F32)],
        compiler_params=pltpu.CompilerParams(vmem_limit_bytes=60 * 2**20),
        )(seg_row, code_col, mixed, mixed, mixed, o, do, lse)


def normed(values, gain_row, shift_row):
    center = values - jnp.mean(values, axis=-1, keepdims=True)
    spread = jnp.mean(center * center, axis=-1, keepdims=True)
    return center * lax.rsqrt(spread + epsilon) * gain_row + shift_row


def gelu_tanh(values):
    return 0.5 * values * (1.0 + jnp.tanh(tanh_scale * (values + 0.044715 * values * values * values)))


def transpose_dot(first_matrix, second_matrix):
    return lax.dot_general(first_matrix, second_matrix, (((0,), (0,)), ((), ())), preferred_element_type=F32)


def dot_transposed(first_matrix, second_matrix):
    return lax.dot_general(first_matrix, second_matrix, (((1,), (1,)), ((), ())), preferred_element_type=F32)


def column_sums(values):
    return jnp.sum(values.astype(F32), axis=0)


LANES = 128


VEC = 4


def norm_rows(values):
    center = values - jnp.mean(values, axis=-1, keepdims=True)
    spread = jnp.mean(center * center, axis=-1, keepdims=True)
    return center * lax.rsqrt(spread + epsilon)


def fill_masks(seg_row, code_row, bias_ref, blocks):
    slot = 0
    turned = [jnp.broadcast_to(code_row[:, b * BQ:(b + 1) * BQ], (BQ, BQ)).T for b in range(blocks)]
    for b in range(blocks):
        low, high = window(b, blocks)
        q = seg_row[:, b * BQ:(b + 1) * BQ]
        for kb in range(low, high):
            ok = turned[kb] == q
            if kb == b:
                ok = ok | (lax.broadcasted_iota(jnp.int32, (BQ, BQ), 0) == lax.broadcasted_iota(jnp.int32, (BQ, BQ), 1))
            bias_ref[slot * BQ:(slot + 1) * BQ, :] = jnp.where(ok, 0.0, NEG)
            slot += 1


def attend_block(b, blocks, q, k, vt, bias_ref, low_rows):
    low, high = window(b, blocks)
    at = slots_before(b, blocks)
    n = high - low
    s = nn(k[low * BQ:high * BQ, :], beside((q * HEAD ** -0.5).T, low_rows))
    bias = bias_ref[at * BQ:(at + n) * BQ, :]
    es, totals, logs = [], [], []
    for h in range(2):
        sh = s[:, h * BQ:(h + 1) * BQ] + bias
        peak = jnp.max(sh, axis=0, keepdims=True)
        e = jnp.exp(sh - peak)
        total = jnp.sum(e, axis=0, keepdims=True)
        es.append(e.astype(BF16))
        totals.append(total)
        logs.append(peak + jnp.log(total))
    ot = nn(vt[:, low * BQ:high * BQ], jnp.concatenate(es, axis=1))
    ot = jnp.concatenate([ot[:HEAD, :BQ] / totals[0], ot[HEAD:, BQ:] / totals[1]], axis=0)
    return ot.T.astype(BF16), jnp.concatenate(logs, axis=1)


F_UNITS = ((4, 0, 128, True), (0, 0, 1152, True), (0, 1152, 2304, False), (1, 0, 384, True), (1, 384, 768, False),
           (2, 0, 1536, True), (2, 1536, 3072, False), (3, 0, 384, True), (3, 384, 768, False))


def picker(lane_of):
    return (lax.broadcasted_iota(jnp.int32, (LANES, lane_of.shape[1]), 0) == lane_of).astype(BF16)


def spread_vectors(table, piece_of, lane_of):
    pieces, count, lanes = table.shape
    found = nn(table.reshape(pieces * count, lanes).astype(BF16), picker(lane_of))
    total = jnp.zeros((count, lane_of.shape[1]), F32)
    for d in range(pieces):
        total = total + jnp.where(piece_of == d, found[d * count:(d + 1) * count], 0.0)
    return total


def spread_vector(rows, piece_of, lane_of):
    found = nn(rows.astype(BF16), picker(lane_of))
    return jnp.sum(jnp.where(lax.broadcasted_iota(jnp.int32, found.shape, 0) == piece_of, found, 0.0), axis=0, keepdims=True)


def forward_kernel(tokens_ref, seg_ref, code_ref, piece_ref, lane_ref, wpiece_ref, wlane_ref,
                   s_qkv, s_proj, s_inner, s_outer, s_vec,
                   g_qkv, g_proj, g_inner, g_outer, ht_hbm, mixed_hbm, attended_hbm, resid_hbm, hidden_two_hbm, lse_ref, vecs_ref, ibias_ref,
                   send, recv, local, vec_buf, wide_ref, w_ref, wp_ref, bias_ref, brow_ref, hidden_ref, ht_ref, mixed_ref, attended_ref, hidden_two_ref, load):
    rows, width = tokens_ref.shape
    blocks = rows // BQ
    pairs = width // (2 * HEAD)
    at = place()
    greet(at)
    srcs, outs = (s_qkv, s_proj, s_inner, s_outer, s_vec), (g_qkv, g_proj, g_inner, g_outer, vec_buf)
    vec, q1, q2, p1, p2, n1, n2, o1, o2 = [
        Gather(u, at, srcs[k], outs[k], slice(a, b), yf, send, recv, local) for u, (k, a, b, yf) in enumerate(F_UNITS)]

    run("start", vec, q1, q2)

    @pl.loop(0, blocks)
    def _(b):
        here = pl.ds(pl.multiple_of(b * BQ, BQ), BQ)
        wide_ref[here, :] = norm_rows(tokens_ref[here, :].astype(F32))

    run("step1", vec, q1, q2)
    run("start", p1, p2, n1, n2)
    fill_masks(seg_ref[...], code_ref[...], bias_ref, blocks)
    run("step2", vec, q1, q2)
    run("step3", vec, q1, q2)
    run("arrive", vec)
    table = vec_buf[...].reshape(32, 16, LANES)
    vecs_ref[...] = spread_vectors(table, piece_ref[...], lane_ref[...])
    ibias_ref[...] = spread_vector(table[:, 8, :], wpiece_ref[...], wlane_ref[...])
    brow_ref[:, :width] = vecs_ref[2:3, :]
    brow_ref[:, width:2 * width] = jnp.zeros((1, width), F32)
    brow_ref[:, 2 * width:] = vecs_ref[3:4, :]

    @pl.loop(0, blocks)
    def _(b):
        here = pl.ds(pl.multiple_of(b * BQ, BQ), BQ)
        hidden_ref[here, :] = (wide_ref[here, :] * vecs_ref[0:1, :] + vecs_ref[1:2, :]).astype(BF16)

    ht_ref[...] = hidden_ref[...].T
    keep = [pltpu.make_async_copy(a, b, load.at[2 + i]) for i, (a, b) in enumerate((
        (ht_ref, ht_hbm), (mixed_ref, mixed_hbm), (attended_ref, attended_hbm), (wide_ref, resid_hbm), (hidden_two_ref, hidden_two_hbm)))]
    keep[0].start()
    run("arrive", q1, q2)
    fetch = pltpu.make_async_copy(g_qkv.reshape(width, 3 * width), w_ref, load.at[0])
    fetch.start()
    run("step1", p1, p2, n1, n2)
    run("start", o1, o2)
    fetch.wait()
    tile = 2 * LANES
    per = width // tile

    @pl.loop(0, 3 * per)
    def _(j):
        cols = pl.ds(pl.multiple_of(j * tile, tile), tile)
        lines = pl.ds(pl.multiple_of(j // per * rows, rows), rows)
        mixed_ref[lines, pl.ds(pl.multiple_of(j % per * tile, tile), tile)] = (nn(hidden_ref[...], w_ref[:, cols]) + brow_ref[:, cols]).astype(BF16)

        @pl.when(j == 4)
        def _():
            run("step2", p1, p2)

        @pl.when(j == 8)
        def _():
            run("step2", n1, n2)

    keep[1].start()
    low_rows = lax.broadcasted_iota(jnp.int32, (2 * HEAD, BQ), 0) < HEAD
    slots = {(0, 3): (("step3", p1, p2),), (0, 7): (("step1", o1, o2),), (1, 7): (("arrive", p1, p2), ("step3", n1, n2)),
             (3, 3): (("step2", o1, o2),), (4, 3): (("arrive", n1, n2),), (5, 3): (("step3", o1, o2),)}

    @pl.loop(0, pairs)
    def _(p):
        cols = pl.ds(pl.multiple_of(p * LANES, LANES), LANES)
        q_ref, k_ref, v_ref = [mixed_ref.at[pl.ds(part * rows, rows), cols] for part in range(3)]
        vt = v_ref[...].T
        for b in range(blocks):
            here = slice(b * BQ, (b + 1) * BQ)
            result, logs = attend_block(b, blocks, q_ref[here, :], k_ref, vt, bias_ref, low_rows)
            attended_ref[here, cols] = result
            lse_ref[p, b:b + 1, :] = logs
            for turn in range(pairs):
                if (turn, b) in slots:
                    @pl.when(p == turn)
                    def _():
                        for name, *units in slots[turn, b]:
                            run(name, *units)

    keep[2].start()
    fetch = pltpu.make_async_copy(g_proj.reshape(width, width), wp_ref, load.at[1])
    fetch.start()
    fetch.wait()

    @pl.loop(0, blocks // 2)
    def _(b):
        here = pl.ds(pl.multiple_of(b * 2 * BQ, 2 * BQ), 2 * BQ)
        resid = tokens_ref[here, :].astype(F32) + nn(attended_ref[here, :], wp_ref[...]) + vecs_ref[4:5, :]
        wide_ref[here, :] = resid
        hidden_two_ref[here, :] = (norm_rows(resid) * vecs_ref[5:6, :] + vecs_ref[6:7, :]).astype(BF16)

    keep[3].start()
    keep[4].start()
    run("arrive", o1, o2)
    for copy in keep:
        copy.wait()
    run("sent", vec, q1, q2, p1, p2, n1, n2, o1, o2)


def forward_part(tokens, seg_row, code_row, qkv, proj, inner, outer, rows16):
    rows, width = tokens.shape
    piece, ff = width // 32, inner.shape[1]
    pairs, blocks = width // (2 * HEAD), rows // BQ
    at, wide_at = jnp.arange(width, dtype=jnp.int32)[None], jnp.arange(ff, dtype=jnp.int32)[None]
    ins = (tokens, seg_row, code_row, at // piece, at % piece, wide_at // (ff // 32), wide_at % (ff // 32), qkv, proj, inner, outer, rows16)
    gathered = [jax.ShapeDtypeStruct((2, 2, 4, 2 * a.shape[0], a.shape[1]), a.dtype) for a in (qkv, proj, inner, outer)]
    made = [jax.ShapeDtypeStruct((width, rows), BF16), jax.ShapeDtypeStruct((3 * rows, width), BF16), jax.ShapeDtypeStruct((rows, width), BF16),
            jax.ShapeDtypeStruct((rows, width), F32), jax.ShapeDtypeStruct((rows, width), BF16)]
    small = [jax.ShapeDtypeStruct((pairs, blocks, 2 * BQ), F32), jax.ShapeDtypeStruct((16, width), F32), jax.ShapeDtypeStruct((1, ff), F32)]
    n = len(F_UNITS)
    out = pl.pallas_call(forward_kernel,
        out_shape=gathered + made + small,
        in_specs=[pl.BlockSpec(memory_space=pltpu.VMEM)] * len(ins),
        out_specs=[pl.BlockSpec(memory_space=pl.ANY)] * 9 + [pl.BlockSpec(memory_space=pltpu.VMEM)] * 3,
        scratch_shapes=[pltpu.SemaphoreType.DMA((n, 8)), pltpu.SemaphoreType.DMA((n, 8)), pltpu.SemaphoreType.DMA((n,)),
                        pltpu.VMEM((2, 2, 4, 32, LANES), F32), pltpu.VMEM((rows, width), F32), pltpu.VMEM((width, 3 * width), BF16),
                        pltpu.VMEM((width, width), BF16), pltpu.VMEM((slots_before(blocks, blocks) * BQ, BQ), F32), pltpu.VMEM((1, 3 * width), F32),
                        pltpu.VMEM((rows, width), BF16), pltpu.VMEM((width, rows), BF16), pltpu.VMEM((3 * rows, width), BF16), pltpu.VMEM((rows, width), BF16),
                        pltpu.VMEM((rows, width), BF16), pltpu.SemaphoreType.DMA((7,))],
        compiler_params=pltpu.CompilerParams(collective_id=0, has_side_effects=True, vmem_limit_bytes=60 * 2**20),
        name="forward_part")(*ins)
    return [g.reshape(-1, g.shape[-1]) for g in out[:4]] + list(out[4:])


CHUNK = 512


def tn(a, b):
    return lax.dot_general(a, b, (((0,), (0,)), ((), ())), preferred_element_type=F32)


def nt(a, b):
    return lax.dot_general(a, b, (((1,), (1,)), ((), ())), preferred_element_type=F32)


class Scatter:
    def __init__(self, unit, at, src, cols, x_first, bufs, send, recv, local, finish):
        x, c, z, y = at
        self.at, self.x_first, self.put = at, x_first, finish
        s = lambda i: (send.at[unit, i], recv.at[unit, i])
        self.mine, self.r0, self.r1, self.r2, self.r3 = mine, r0, r1, r2, r3 = bufs
        rows = mine.shape[3]
        grad = lambda cc, yy: src.at[:, cc, :, pl.ds(yy * rows, rows), cols]
        core, ydev, xdev = device(x, 1 - c, z, y), device(x, c, z, 1 - y), device(1 - x, c, z, y)
        self.load = [pltpu.make_async_copy(grad(c, yy), mine.at[:, :, yy], local.at[unit, yy]) for yy in range(2)]
        self.c0 = [remote(grad(1 - c, yy), r0.at[:, :, yy], *s(yy), core) for yy in range(2)]
        if x_first:
            self.c1 = remote(mine.at[1 - x], r1, *s(2), xdev)
            self.c2 = remote(mine.at[x, :, 1 - y], r2, *s(3), ydev)
        else:
            self.c1 = remote(mine.at[:, :, 1 - y], r1, *s(2), ydev)
            self.c2 = remote(mine.at[1 - x, :, y], r2, *s(3), xdev)
        self.z = [remote(mine.at[x, (z + d + 1) % 4, y], r3.at[d], *s(4 + d), device(x, c, (z + d + 1) % 4, y)) for d in range(3)]

    def start(self):
        for copy in self.c0 + self.load:
            copy.start()

    def add(self, target, other):
        target[...] = (target[...].astype(F32) + other[...].astype(F32)).astype(target.dtype)

    def step1(self):
        for copy in self.load:
            copy.wait()
        for copy in self.c0:
            copy.wait_recv()

        @pl.loop(0, 16)
        def _(j):
            i = (j // 8, (j // 2) % 4, j % 2)
            self.add(self.mine.at[i], self.r0.at[i])

        self.c1.start()

    def step2(self):
        x, c, z, y = self.at
        self.c1.wait_recv()

        @pl.loop(0, 8)
        def _(j):
            if self.x_first:
                self.add(self.mine.at[x, j // 2, j % 2], self.r1.at[j // 2, j % 2])
            else:
                self.add(self.mine.at[j // 4, j % 4, y], self.r1.at[j // 4, j % 4])

        self.c2.start()

    def step3(self):
        x, c, z, y = self.at
        self.c2.wait_recv()

        @pl.loop(0, 4)
        def _(j):
            self.add(self.mine.at[x, j, y], self.r2.at[j])

        for copy in self.z:
            copy.start()

    def finish(self):
        x, c, z, y = self.at
        for copy in self.z:
            copy.wait_recv()
        total = self.mine[x, z, y].astype(F32)
        for d in range(3):
            total = total + self.r3[d].astype(F32)
        self.put(total)

    def sent(self):
        for copy in self.c0 + [self.c1, self.c2] + self.z:
            copy.wait_send()


def run(name, *units):
    for unit in units:
        getattr(unit, name)()


def norm_back(values, grads, gain):
    center = values - jnp.mean(values, axis=-1, keepdims=True)
    r = lax.rsqrt(jnp.mean(center * center, axis=-1, keepdims=True) + epsilon)
    n = center * r
    t = grads * gain
    back = r * (t - jnp.mean(t, axis=-1, keepdims=True) - n * jnp.mean(t * n, axis=-1, keepdims=True))
    return back, jnp.sum(grads * n, axis=0, keepdims=True), jnp.sum(grads, axis=0, keepdims=True)


def backward_pair(q_ref, k_ref, v_ref, o_ref, do_ref, logs, bias_ref, dk_acc, dv_acc, blocks, low_rows, low_cols):
    kt = k_ref[...].T
    dk_acc[...] = jnp.zeros_like(dk_acc)
    dv_acc[...] = jnp.zeros_like(dv_acc)

    def stack(x):
        zero = jnp.zeros_like(x)
        return jnp.concatenate([jnp.where(low_cols, x, zero), jnp.where(low_cols, zero, x)], axis=0)

    for b in range(blocks):
        low, high = window(b, blocks)
        at = slots_before(b, blocks)
        here = slice(b * BQ, (b + 1) * BQ)
        keys = slice(low * BQ, high * BQ)
        q = q_ref[here, :] * HEAD ** -0.5
        do = do_ref[here, :]
        dprod = (do.astype(F32) * o_ref[here, :].astype(F32)).T
        s = nn(k_ref[keys, :], beside(q.T, low_rows))
        dp = nn(v_ref[keys, :], beside(do.T, low_rows))
        bias = bias_ref[at * BQ:(at + high - low) * BQ, :]
        ps, ds = [], []
        for h in range(2):
            cols = slice(h * BQ, (h + 1) * BQ)
            p = jnp.exp(s[:, cols] + bias - logs[b:b + 1, cols])
            delta = jnp.sum(dprod[h * HEAD:(h + 1) * HEAD], axis=0, keepdims=True)
            ds.append((p * (dp[:, cols] - delta)).astype(BF16))
            ps.append(p.astype(BF16))
        ds2 = jnp.concatenate(ds, axis=1)
        dv_acc[keys, :] += nn(jnp.concatenate(ps, axis=1), stack(do))
        dk_acc[keys, :] += nn(ds2, stack(q))
        dqt = nn(kt[:, keys], ds2)
        dqt = jnp.concatenate([dqt[:HEAD, :BQ], dqt[HEAD:, BQ:]], axis=0) * HEAD ** -0.5
        q_ref[here, :] = dqt.T.astype(BF16)
    k_ref[...] = dk_acc[...].astype(BF16)
    v_ref[...] = dv_acc[...].astype(BF16)


B_UNITS = tuple((2, i * CHUNK, (i + 1) * CHUNK, i % 2 == 0) for i in range(6)) + (
    (3, 0, 384, True), (3, 384, 768, False), (1, 0, 384, True), (1, 384, 768, False),
    (0, 0, 1152, True), (0, 1152, 1792, False), (0, 1792, 2304, True), (4, 0, 128, True))


def backward_kernel(seg_ref, code_ref, piece_ref, lane_ref, wpiece_ref, wlane_ref, vecs_ref, ibias_ref, lse_ref, h2_hbm, cot_hbm,
                    tokens_hbm, resid_hbm, mixed_hbm, attended_hbm, h1t_hbm, w_qkv, w_proj, w_inner, w_outer,
                    out_ref, gtok_ref, s_qkv, s_proj, s_inner, s_outer, s_vec, g_qkv, g_proj, g_inner, g_outer, g_vec,
                    send, recv, local, load, stage, h2_ref, cot_ref, a_ref, b_ref, ht_ref, acc1, acc2, resid_ref, act_ref, dpre_ref, sto, sti, att_ref,
                    bias_ref, dk_acc, dv_acc, sums, isum, vst, *bufs):
    rows, width = h2_ref.shape
    ff = ibias_ref.shape[1]
    blocks, pairs, chunks = rows // BQ, width // (2 * HEAD), ff // CHUNK
    at = place()
    greet(at)
    split = lambda ref: ref.reshape(2, 2, 4, ref.shape[0] // 16, ref.shape[1])
    grads = [split(g) for g in (g_qkv, g_proj, g_inner, g_outer)] + [g_vec]

    def put(ref, first, last):
        def write(total):
            ref[:, first:last] = total
        return write

    def put_pairs(first, last):
        def write(total):
            for tile in range(first // LANES, last // LANES):
                to = (tile % 3) * width + tile // 3 * LANES
                s_qkv[:, to:to + LANES] = total[:, tile * LANES - first:(tile + 1) * LANES - first]
        return write

    shares = (None, s_proj, s_inner, s_outer, s_vec)
    units = [Scatter(u, at, grads[k], slice(a, b), xf, bufs[5 * u:5 * u + 5], send, recv, local,
                     put_pairs(a, b) if k == 0 else put(shares[k], a, b)) for u, (k, a, b, xf) in enumerate(B_UNITS)]
    n, o, p, (q1, q2, q3), v = units[:6], units[6:8], units[8:10], units[10:13], units[13]

    tile = lambda ref, i, size: ref.at[:, pl.ds(pl.multiple_of(i * size, size), size)]
    band = lambda ref, i, size: ref.at[pl.ds(pl.multiple_of(i * size, size), size)]
    load_inner = lambda i: pltpu.make_async_copy(tile(w_inner, i, CHUNK), tile(b_ref, i, CHUNK), load.at[i])
    load_outer = lambda i: pltpu.make_async_copy(band(w_outer, i, CHUNK), band(a_ref, i, CHUNK), load.at[chunks + i])
    more = 2 * chunks
    load_resid = pltpu.make_async_copy(resid_hbm, resid_ref, load.at[more])
    load_att = pltpu.make_async_copy(attended_hbm, att_ref, load.at[more + 1])
    load_wp = pltpu.make_async_copy(w_proj, b_ref.at[:, 3 * width:], load.at[more + 2])
    load_wq = pltpu.make_async_copy(w_qkv, b_ref.at[:, :3 * width], load.at[more + 3])
    load_mixed = pltpu.make_async_copy(mixed_hbm, a_ref, load.at[more + 4])
    load_ht = pltpu.make_async_copy(h1t_hbm, ht_ref, load.at[more + 5])
    load_tok = pltpu.make_async_copy(tokens_hbm, att_ref, load.at[more + 6])
    out_inner = lambda i: pltpu.make_async_copy(sti.at[i % 2], tile(g_inner, i, CHUNK), stage.at[i % 2])
    out_outer = lambda i: pltpu.make_async_copy(sto.at[i % 2], band(g_outer, i, CHUNK), stage.at[2 + i % 2])

    load_h2 = pltpu.make_async_copy(h2_hbm, h2_ref, load.at[more + 7])
    load_cot = pltpu.make_async_copy(cot_hbm, cot_ref, load.at[more + 8])
    load_h2.start()
    load_cot.start()
    for i in range(chunks):
        load_inner(i).start()
        load_outer(i).start()
    load_resid.start()
    load_att.start()
    acc1[...] = jnp.zeros_like(acc1)
    acc2[...] = jnp.zeros_like(acc2)
    sums[...] = jnp.zeros_like(sums)
    load_h2.wait()
    ht_ref[...] = h2_ref[...].T
    load_cot.wait()
    fill_masks(seg_ref[...], code_ref[...], bias_ref, blocks)

    @pl.loop(0, chunks)
    def _(i):
        cols = pl.ds(pl.multiple_of(i * CHUNK, CHUNK), CHUNK)
        load_inner(i).wait()
        load_outer(i).wait()

        @pl.loop(0, rows // (2 * BQ))
        def _(rb):
            here = pl.ds(pl.multiple_of(rb * 2 * BQ, 2 * BQ), 2 * BQ)
            x = nn(h2_ref[here, :], b_ref[:, cols]) + ibias_ref[:, cols]
            d_act = nt(cot_ref[here, :], a_ref[cols, :])
            x2 = x * x
            half = 0.5 + 0.5 * jnp.tanh(x * (tanh_scale + tanh_scale * 0.044715 * x2))
            act = (x * half).astype(BF16)
            slope = half + half * (1.0 - half) * x * (2.0 * tanh_scale + 6.0 * tanh_scale * 0.044715 * x2)
            d_pre = (d_act * slope).astype(BF16)
            act_ref[here, :] = act
            dpre_ref[here, :] = d_pre
            acc1[here, :] += nn(act, a_ref[cols, :])
            acc2[here, :] += nt(d_pre, b_ref[:, cols])

        isum[:, cols] = jnp.sum(dpre_ref[...].astype(F32), axis=0, keepdims=True)

        @pl.when(i >= 1)
        def _():
            out_inner(i - 1).wait()
            out_outer(i - 1).wait()

        sto[i % 2] = tn(act_ref[...], cot_ref[...]).astype(BF16)
        sti[i % 2] = nn(ht_ref[...], dpre_ref[...]).astype(BF16)
        out_inner(i).start()
        out_outer(i).start()
        for turn in range(1, chunks):
            @pl.when(i == turn)
            def _():
                for name, lag in (("start", 1), ("step1", 2), ("step2", 3), ("step3", 4), ("finish", 5)):
                    if turn >= lag:
                        run(name, n[turn - lag])

    load_mixed.start()
    load_ht.start()
    load_wp.start()
    load_wq.start()
    out_inner(chunks - 1).wait()
    out_outer(chunks - 1).wait()
    run("start", n[5], *o)
    run("step1", n[4])
    run("step2", n[3])
    run("step3", n[2])
    run("finish", n[1])
    load_resid.wait()

    @pl.loop(0, blocks)
    def _(b):
        here = pl.ds(pl.multiple_of(b * BQ, BQ), BQ)
        resid = resid_ref[here, :]
        out_ref[here, :] = (resid + acc1[here, :] + vecs_ref[7:8, :]).astype(BF16)
        cot = cot_ref[here, :].astype(F32)
        back, gain, shift = norm_back(resid, acc2[here, :], vecs_ref[5:6, :])
        d_resid = cot + back
        acc1[here, :] = d_resid
        branch = d_resid.astype(BF16)
        h2_ref[here, :] = branch
        sums[4:5, :] += jnp.sum(branch.astype(F32), axis=0, keepdims=True)
        sums[5:6, :] += gain
        sums[6:7, :] += shift
        sums[7:8, :] += jnp.sum(cot, axis=0, keepdims=True)

    load_wp.wait()
    load_att.wait()

    @pl.loop(0, rows // (2 * BQ))
    def _(rb):
        here = pl.ds(pl.multiple_of(rb * 2 * BQ, 2 * BQ), 2 * BQ)
        cot_ref[here, :] = nt(h2_ref[here, :], b_ref[:, 3 * width:]).astype(BF16)

    run("step1", n[5])
    run("step2", n[4])
    run("step3", n[3])
    run("finish", n[2])
    part = tn(att_ref[...], h2_ref[...]).astype(BF16)
    sto[0, :width // 2, :] = part[:width // 2]
    sto[1, :width // 2, :] = part[width // 2:]
    out_proj = [pltpu.make_async_copy(sto.at[i, :width // 2], band(g_proj, i, width // 2), stage.at[2 + i]) for i in range(2)]
    for copy in out_proj:
        copy.start()
    run("step1", *o)
    load_mixed.wait()
    load_ht.wait()
    low_rows = lax.broadcasted_iota(jnp.int32, (2 * HEAD, BQ), 0) < HEAD
    low_cols = lax.broadcasted_iota(jnp.int32, (BQ, 2 * HEAD), 1) < HEAD
    for copy in out_proj:
        copy.wait()
    run("start", *p)
    out_pair = lambda i: pltpu.make_async_copy(sti.at[i % 2, :, :3 * LANES], tile(g_qkv, i, 3 * LANES), stage.at[i % 2])
    turns = {0: (("step2", n[5]), ("step3", n[4]), ("finish", n[3])),
             1: (("step2", *o), ("step1", *p), ("step3", n[5]), ("finish", n[4])),
             2: (("step2", *p), ("finish", n[5])),
             3: (("start", q1), ("step3", *o)),
             4: (("step1", q1), ("step3", *p), ("finish", *o)),
             5: (("step2", q1), ("finish", *p))}

    @pl.loop(0, pairs)
    def _(i):
        cols = pl.ds(pl.multiple_of(i * LANES, LANES), LANES)
        three = [a_ref.at[pl.ds(part * rows, rows), cols] for part in range(3)]
        backward_pair(*three, att_ref.at[:, cols], cot_ref.at[:, cols], lse_ref.at[i], bias_ref, dk_acc, dv_acc, blocks, low_rows, low_cols)
        sums[2:3, cols] = jnp.sum(three[0][...].astype(F32), axis=0, keepdims=True)
        sums[3:4, cols] = jnp.sum(three[2][...].astype(F32), axis=0, keepdims=True)

        @pl.when(i >= 1)
        def _():
            out_pair(i - 1).wait()

        sti[i % 2, :, :3 * LANES] = nn(ht_ref[...], jnp.concatenate([ref[...] for ref in three], axis=1)).astype(BF16)
        out_pair(i).start()
        for turn in range(pairs):
            @pl.when(i == turn)
            def _():
                for name, *some in turns[turn]:
                    run(name, *some)

    load_tok.start()
    out_pair(pairs - 1).wait()
    run("start", q2, q3)
    load_wq.wait()
    load_tok.wait()
    run("step3", q1)

    @pl.loop(0, rows // (2 * BQ))
    def _(rb):
        here = pl.ds(pl.multiple_of(rb * 2 * BQ, 2 * BQ), 2 * BQ)
        total = nt(a_ref[here, :], b_ref[:, :width])
        for part in range(1, 3):
            lines = pl.ds(pl.multiple_of(rb * 2 * BQ + part * rows, 2 * BQ), 2 * BQ)
            total = total + nt(a_ref[lines, :], b_ref[:, part * width:(part + 1) * width])
        acc2[here, :] = total

        @pl.when(rb == 2)
        def _():
            run("step1", q2, q3)

    run("step2", q2, q3)

    @pl.loop(0, blocks)
    def _(b):
        here = pl.ds(pl.multiple_of(b * BQ, BQ), BQ)
        back, gain, shift = norm_back(att_ref[here, :].astype(F32), acc2[here, :], vecs_ref[0:1, :])
        gtok_ref[here, :] = (acc1[here, :] + back).astype(BF16)
        sums[0:1, :] += gain
        sums[1:2, :] += shift

    pick, wide_pick = picker(lane_ref[...]), picker(wlane_ref[...])
    shard = lax.broadcasted_iota(jnp.int32, (32, width), 0)
    for k in range(8):
        piece = nt(jnp.where(shard == piece_ref[...], sums[k:k + 1, :], 0.0).astype(BF16), pick)
        vst[:, k, :] = piece
    shard = lax.broadcasted_iota(jnp.int32, (32, ff), 0)
    vst[:, 8, :] = nt(jnp.where(shard == wpiece_ref[...], isum[...], 0.0).astype(BF16), wide_pick)
    out_vec = pltpu.make_async_copy(vst.reshape(2, 2, 4, 32, LANES), g_vec, stage.at[0])
    out_vec.start()
    out_vec.wait()
    run("start", v)
    run("step3", q2, q3)
    run("step1", v)
    run("finish", q1)
    run("step2", v)
    run("finish", q2, q3)
    run("step3", v)
    run("finish", v)
    run("sent", *units)


def backward_part(tokens, seg_row, code_row, cotangent, qkv, proj, inner, outer, h1t, mixed, attended, log_total, resid, hidden_two, vecs, ibias):
    rows, width = tokens.shape
    ff = inner.shape[1]
    piece = width // 32
    blocks = rows // BQ
    at, wide_at = jnp.arange(width, dtype=jnp.int32)[None], jnp.arange(ff, dtype=jnp.int32)[None]
    fast = (seg_row, code_row, at // piece, at % piece, wide_at // (ff // 32), wide_at % (ff // 32), vecs, ibias, log_total)
    slow = (hidden_two, cotangent, tokens, resid, mixed, attended, h1t, qkv, proj, inner, outer)
    vmem, anywhere = pl.BlockSpec(memory_space=pltpu.VMEM), pl.BlockSpec(memory_space=pl.ANY)
    shares = [jax.ShapeDtypeStruct((a.shape[0] // 32, a.shape[1]), F32) for a in (qkv, proj, inner, outer)] + [jax.ShapeDtypeStruct((16, LANES), F32)]
    whole = [jax.ShapeDtypeStruct(a.shape, BF16) for a in (qkv, proj, inner, outer)] + [jax.ShapeDtypeStruct((2, 2, 4, 32, LANES), F32)]
    bufs = []
    for k, a, b, xf in B_UNITS:
        block = (shares[k].shape[0], b - a)
        for lead in ((2, 4, 2), (2, 4, 2), (4, 2) if xf else (2, 4), (4,), (3,)):
            bufs.append(pltpu.VMEM(lead + block, whole[k].dtype))
    n = len(B_UNITS)
    out = pl.pallas_call(backward_kernel,
        out_shape=[jax.ShapeDtypeStruct((rows, width), BF16)] * 2 + shares + whole,
        in_specs=[vmem] * len(fast) + [anywhere] * len(slow),
        out_specs=[vmem] * 7 + [anywhere] * 5,
        scratch_shapes=[pltpu.SemaphoreType.DMA((n, 7)), pltpu.SemaphoreType.DMA((n, 7)), pltpu.SemaphoreType.DMA((n, 2)), pltpu.SemaphoreType.DMA((2 * (ff // CHUNK) + 9,)), pltpu.SemaphoreType.DMA((4,)),
                        pltpu.VMEM((rows, width), BF16), pltpu.VMEM((rows, width), BF16), pltpu.VMEM((3 * rows, width), BF16), pltpu.VMEM((width, ff), BF16), pltpu.VMEM((width, rows), BF16),
                        pltpu.VMEM((rows, width), F32), pltpu.VMEM((rows, width), F32), pltpu.VMEM((rows, width), F32),
                        pltpu.VMEM((rows, CHUNK), BF16), pltpu.VMEM((rows, CHUNK), BF16), pltpu.VMEM((2, CHUNK, width), BF16), pltpu.VMEM((2, width, CHUNK), BF16),
                        pltpu.VMEM((rows, width), BF16), pltpu.VMEM((slots_before(blocks, blocks) * BQ, BQ), F32),
                        pltpu.VMEM((rows, LANES), F32), pltpu.VMEM((rows, LANES), F32), pltpu.VMEM((8, width), F32), pltpu.VMEM((1, ff), F32), pltpu.VMEM((32, 16, LANES), F32)] + bufs,
        compiler_params=pltpu.CompilerParams(collective_id=1, has_side_effects=True, vmem_limit_bytes=67043328),
        name="backward_part")(*fast, *slow)
    return out[:7]


def pack_rows(parts, shards):
    piece = parts[0].shape[0] // shards
    rows = jnp.concatenate([part.reshape(shards, -1, piece) for part in parts], axis=1)
    rows = jnp.pad(rows, ((0, 0), (0, 16 - rows.shape[1]), (0, LANES - piece)))
    return rows.reshape(shards * 16, LANES)


def unpack_rows(rows, piece, counts):
    table = rows.reshape(-1, 16, LANES)[:, :, :piece]
    parts, at = [], 0
    for count in counts:
        parts.append(table[:, at : at + count].reshape(-1))
        at += count
    return parts


def solution(mesh):
    by_chip = mesh.shape["dp"] == 4 and mesh.shape["fsdp"] == 8
    shards = mesh.shape["dp"] * mesh.shape["fsdp"]

    def gather_all(*arrays):
        return tuple(lax.all_gather(a, AXES, axis=0, tiled=True) for a in arrays)

    def scatter_all(*arrays):
        return tuple(lax.psum_scatter(a.astype(F32), AXES, scatter_dimension=0, tiled=True) for a in arrays)

    def by_kernels(tokens, segment_ids, live_mask, cotangent, qkv_weight, proj_weight, inner_weight, outer_weight, vectors):
        piece = vectors[0].shape[0]
        rows16 = jnp.stack([jnp.pad(v.astype(F32), (0, LANES - v.shape[0])) for v in vectors])
        rows16 = jnp.pad(rows16, ((0, 16 - rows16.shape[0]), (0, 0)))
        seg_row = segment_ids[None, :]
        code_row = jnp.where(live_mask == 1, segment_ids, -1)[None, :]
        qkv, proj, inner, outer, h1t, mixed, attended, resid, hidden_two, log_total, vecs, ibias = forward_part(
            tokens, seg_row, code_row, qkv_weight, proj_weight, inner_weight, outer_weight, rows16)
        layer_out, grad_tokens, s_qkv, s_proj, s_inner, s_outer, s_rows = backward_part(
            tokens, seg_row, code_row, cotangent, qkv, proj, inner, outer, h1t, mixed, attended, log_total, resid, hidden_two, vecs, ibias)
        g1, s1, gq, gv, gp, g2, s2, go = [s_rows[k, :piece] for k in range(8)]
        gi = s_rows[8, :vectors[8].shape[0]]
        return (layer_out, grad_tokens, g1, s1, s_qkv, gq, gv, s_proj, gp, g2, s2, s_inner, gi, s_outer, go)

    def per_device(tokens, segment_ids, live_mask, cotangent, first_gain, first_shift, qkv_weight, query_bias, value_bias,
                   proj_weight, proj_bias, second_gain, second_shift, inner_weight, inner_bias, outer_weight, outer_bias):
        piece = first_gain.shape[0]
        vectors = (first_gain, first_shift, query_bias, value_bias, proj_bias, second_gain, second_shift, outer_bias, inner_bias)
        counts = tuple(v.shape[0] // piece for v in vectors)
        if by_chip:
            return by_kernels(tokens, segment_ids, live_mask, cotangent, qkv_weight, proj_weight, inner_weight, outer_weight, vectors)
        qkv, proj, inner, outer, rows = gather_all(qkv_weight, proj_weight, inner_weight, outer_weight, pack_rows(vectors, 1))
        gain_one, shift_one, qbias, vbias, pbias, gain_two, shift_two, obias, ibias = (
            v.astype(F32) for v in unpack_rows(rows, piece, counts))
        seg_row = segment_ids[None, :]
        code_col = jnp.where(live_mask == 1, segment_ids, -1)[:, None]
        wide = tokens.astype(F32)
        normed_one, first_pull = jax.vjp(normed, wide, gain_one, shift_one)
        hidden_one = normed_one.astype(BF16)
        bias_row = jnp.concatenate([qbias, jnp.zeros_like(qbias), vbias])
        mixed = (jnp.dot(hidden_one, qkv, preferred_element_type=F32) + bias_row).astype(BF16)
        attended, log_total = attn_fwd(seg_row, code_col, mixed)
        resid = wide + jnp.dot(attended, proj, preferred_element_type=F32) + pbias
        normed_two, second_pull = jax.vjp(normed, resid, gain_two, shift_two)
        hidden_two = normed_two.astype(BF16)
        pre = jnp.dot(hidden_two, inner, preferred_element_type=F32) + ibias
        act_wide, gelu_pull = jax.vjp(gelu_tanh, pre)
        act = act_wide.astype(BF16)
        layer_out = (resid + jnp.dot(act, outer, preferred_element_type=F32) + obias).astype(BF16)
        cot_wide = cotangent.astype(F32)
        grad_outer = transpose_dot(act, cotangent).astype(BF16)
        d_pre = gelu_pull(dot_transposed(cotangent, outer))[0].astype(BF16)
        grad_inner = transpose_dot(hidden_two, d_pre).astype(BF16)
        d_resid_norm, grad_gain_two, grad_shift_two = second_pull(dot_transposed(d_pre, inner))
        d_resid = cot_wide + d_resid_norm
        d_branch = d_resid.astype(BF16)
        grad_proj = transpose_dot(attended, d_branch).astype(BF16)
        d_attended = dot_transposed(d_branch, proj).astype(BF16)
        d_query, d_key, d_value = attn_bwd(seg_row, code_col, mixed, attended, d_attended, log_total)
        d_mixed = jnp.concatenate([d_query, d_key, d_value], axis=1)
        grad_qkv = transpose_dot(hidden_one, d_mixed).astype(BF16)
        d_tokens_norm, grad_gain_one, grad_shift_one = first_pull(dot_transposed(d_mixed, qkv))
        grad_tokens = (d_resid + d_tokens_norm).astype(BF16)
        sums = (grad_gain_one, grad_shift_one, column_sums(d_query), column_sums(d_value), column_sums(d_branch),
                grad_gain_two, grad_shift_two, jnp.sum(cot_wide, axis=0), column_sums(d_pre))
        s_qkv, s_proj, s_inner, s_outer, s_rows = scatter_all(
            grad_qkv, grad_proj, grad_inner, grad_outer, pack_rows(sums, shards).astype(BF16))
        g1, s1, gq, gv, gp, g2, s2, go, gi = unpack_rows(s_rows, piece, counts)
        return (layer_out, grad_tokens, g1, s1, s_qkv, gq, gv, s_proj, gp, g2, s2, s_inner, gi, s_outer, go)

    flat, matrix = P(AXES), P(AXES, None)
    return jax.shard_map(
        per_device,
        mesh=mesh,
        in_specs=(matrix, flat, flat, matrix, flat, flat, matrix, flat, flat, matrix, flat, flat, flat, matrix, flat, matrix, flat),
        out_specs=(matrix, matrix, flat, flat, matrix, flat, flat, matrix, flat, flat, flat, matrix, flat, matrix, flat),
        check_vma=False,
    )
```

profile of v0, /device:TPU:0, one launch (start us, length us, event | category | flops | bytes accessed | tf_op | source)
XLA Modules:
  0.0 260.6 jit_solution(5925998763883535436)
XLA Ops:
  0.6 0.7 pad_bitcast_fusion.8
  1.3 0.7 pad_bitcast_fusion.6
  2.0 0.7 pad_bitcast_fusion.4
  2.7 0.7 pad_bitcast_fusion.2
  3.3 0.7 pad_bitcast_fusion
  4.0 0.1 stack.49
  4.1 0.6 pad_convert_fusion.s_vec
  4.7 1.3 compare_select_fusion
  6.0 0.6 and_select_fusion.2
  6.6 0.6 and_select_fusion
  7.2 94.6 %forward_part.1 = (bf16[2,2,4,48,2304]{4,3,2,1,0:T(8,128)(2,1)}, bf16[2,2,4,48,768]{4,3,2,1,0:T(8,128)(2,1)}, bf16[2,2,4,48,3072]{4,3,2,1,0:T(8,128)(2,1)}, bf16...) custom-call(bf16[1024,768]{1,0:T(8,128)(2,1)} %tokens_hbm.1, ...), custom_call_target="tpu_custom_call" | custom-call | tf_op jit(solution)/shard_map/forward_part/pallas_call | solution.py:425
  101.8 149.4 %backward_part.1 = (bf16[1024,768]{1,0:T(8,128)(2,1)}, bf16[1024,768]{1,0:T(8,128)(2,1)}, f32[24,2304]{1,0:T(8,128)}, f32[24,768]{1,0:T(8,128)}, f32[24,3072]{1,...) custom-call(s32[1,1024]{1,0:T(1,128)} %bitcast.47, ...), custom_call_target="tpu_custom_call" | custom-call | tf_op jit(solution)/shard_map/backward_part/pallas_call | solution.py:835
  251.2 1.2 slice_bitcast_fusion.1
  252.4 1.5 slice_bitcast_fusion
  253.9 0.0 copy-start
  253.9 2.8 %copy.38 = bf16[1024,768]{1,0:T(8,128)(2,1)} copy(bf16[1024,768]{1,0:T(8,128)(2,1)} %get-tuple-element.88) | data formatting | bytes 3145728
  256.7 0.0 copy-done
  256.7 0.0 copy-start.3
  256.7 0.0 copy-start.4
  256.7 0.0 copy-start.2
  256.7 0.0 copy-start.1
  256.7 1.1 copy.39
  257.8 0.0 copy-done.3
  257.9 0.7 copy.40
  258.5 0.0 copy-done.4
  258.5 0.6 copy.41
  259.2 0.0 copy-done.2
  259.2 0.7 copy.42
  259.9 0.0 copy-done.1
  259.9 0.7 copy.43
Async XLA Ops:
  253.9 2.8 %copy-start = (bf16[1024,768]{1,0:T(8,128)(2,1)S(1)}, bf16[1024,768]{1,0:T(8,128)(2,1)}, u32[]{:S(2)}) copy-start(bf16[1024,768]{1,0:T(8,128)(2,1)} %get-tuple-element.89) | copy-start | bytes 4718596
  256.7 1.2 copy-start.3
  256.7 1.9 copy-start.4
  256.7 2.5 copy-start.2
  256.7 3.2 %copy-start.1 = (f32[96,768]{1,0:T(8,128)S(1)}, f32[96,768]{1,0:T(8,128)}, u32[]{:S(2)}) copy-start(f32[96,768]{1,0:T(8,128)} %get-tuple-element.101) | copy-start | bytes 884740
where the time goes:
time: 261 us
  Pallas kernels  244 us (93%)
  local copies, waits for them, and re-layouts  12.8 us (5%)
  other arithmetic  3.14 us (1%)
    pallas_call x1, Pallas kernels, backward_part(): pl.pallas_call(backward_kernel, out_shape=[jax.ShapeDtypeStruct((rows, wi...  149 us
    pallas_call x1, Pallas kernels, forward_part(): pl.pallas_call(forward_kernel, out_shape=gathered + made + small, in_spec...  94.6 us
    unnamed x16, local copies, waits for them, and re-layouts  6.68 us

commit v1 on v0

--- a/solution.py
+++ b/solution.py
@@ -1,5 +1,6 @@
 import jax
 import jax.numpy as jnp
+import numpy as np
 from jax import lax
 from jax.experimental import pallas as pl
 from jax.experimental.pallas import tpu as pltpu
@@ -282,7 +283,7 @@
     return ot.T.astype(BF16), jnp.concatenate(logs, axis=1)
 
 
-F_UNITS = ((4, 0, 128, True), (0, 0, 1152, True), (0, 1152, 2304, False), (1, 0, 384, True), (1, 384, 768, False),
+F_UNITS = ((4, 0, 128, True), (0, 0, 640, True), (0, 640, 1152, False), (0, 1152, 1792, True), (0, 1792, 2304, False), (1, 0, 384, True), (1, 384, 768, False),
            (2, 0, 1536, True), (2, 1536, 3072, False), (3, 0, 384, True), (3, 384, 768, False))
 
 
@@ -314,21 +315,23 @@
     at = place()
     greet(at)
     srcs, outs = (s_qkv, s_proj, s_inner, s_outer, s_vec), (g_qkv, g_proj, g_inner, g_outer, vec_buf)
-    vec, q1, q2, p1, p2, n1, n2, o1, o2 = [
-        Gather(u, at, srcs[k], outs[k], slice(a, b), yf, send, recv, local) for u, (k, a, b, yf) in enumerate(F_UNITS)]
-
-    run("start", vec, q1, q2)
+    units = [Gather(u, at, srcs[k], outs[k], slice(a, b), yf, send, recv, local) for u, (k, a, b, yf) in enumerate(F_UNITS)]
+    vec, early, late, p, n, o = units[0], units[1:3], units[3:5], units[5:7], units[7:9], units[9:11]
+
+    run("start", vec, *early, *late)
 
     @pl.loop(0, blocks)
     def _(b):
         here = pl.ds(pl.multiple_of(b * BQ, BQ), BQ)
         wide_ref[here, :] = norm_rows(tokens_ref[here, :].astype(F32))
 
-    run("step1", vec, q1, q2)
-    run("start", p1, p2, n1, n2)
+    run("step1", vec, *early)
+    run("step2", vec, *early)
+    run("step1", *late)
+    run("start", *p, *n)
     fill_masks(seg_ref[...], code_ref[...], bias_ref, blocks)
-    run("step2", vec, q1, q2)
-    run("step3", vec, q1, q2)
+    run("step2", *late)
+    run("step3", vec, *early)
     run("arrive", vec)
     table = vec_buf[...].reshape(32, 16, LANES)
     vecs_ref[...] = spread_vectors(table, piece_ref[...], lane_ref[...])
@@ -346,11 +349,12 @@
     keep = [pltpu.make_async_copy(a, b, load.at[2 + i]) for i, (a, b) in enumerate((
         (ht_ref, ht_hbm), (mixed_ref, mixed_hbm), (attended_ref, attended_hbm), (wide_ref, resid_hbm), (hidden_two_ref, hidden_two_hbm)))]
     keep[0].start()
-    run("arrive", q1, q2)
+    run("step3", *late)
+    run("arrive", *early, *late)
     fetch = pltpu.make_async_copy(g_qkv.reshape(width, 3 * width), w_ref, load.at[0])
     fetch.start()
-    run("step1", p1, p2, n1, n2)
-    run("start", o1, o2)
+    run("step1", *p, *n)
+    run("start", *o)
     fetch.wait()
     tile = 2 * LANES
     per = width // tile
@@ -361,32 +365,28 @@
         lines = pl.ds(pl.multiple_of(j // per * rows, rows), rows)
         mixed_ref[lines, pl.ds(pl.multiple_of(j % per * tile, tile), tile)] = (nn(hidden_ref[...], w_ref[:, cols]) + brow_ref[:, cols]).astype(BF16)
 
-        @pl.when(j == 4)
-        def _():
-            run("step2", p1, p2)
-
         @pl.when(j == 8)
         def _():
-            run("step2", n1, n2)
+            run("step2", *p)
 
     keep[1].start()
     low_rows = lax.broadcasted_iota(jnp.int32, (2 * HEAD, BQ), 0) < HEAD
-    slots = {(0, 3): (("step3", p1, p2),), (0, 7): (("step1", o1, o2),), (1, 7): (("arrive", p1, p2), ("step3", n1, n2)),
-             (3, 3): (("step2", o1, o2),), (4, 3): (("arrive", n1, n2),), (5, 3): (("step3", o1, o2),)}
+    slots = {(0, 3): (("step2", *n),), (1, 7): (("step1", *o),), (2, 3): (("step3", *p),), (4, 3): (("arrive", *p),),
+             (4, 7): (("step3", *n),), (5, 3): (("step2", *o),)}
 
     @pl.loop(0, pairs)
-    def _(p):
-        cols = pl.ds(pl.multiple_of(p * LANES, LANES), LANES)
+    def _(pair):
+        cols = pl.ds(pl.multiple_of(pair * LANES, LANES), LANES)
         q_ref, k_ref, v_ref = [mixed_ref.at[pl.ds(part * rows, rows), cols] for part in range(3)]
         vt = v_ref[...].T
         for b in range(blocks):
             here = slice(b * BQ, (b + 1) * BQ)
             result, logs = attend_block(b, blocks, q_ref[here, :], k_ref, vt, bias_ref, low_rows)
             attended_ref[here, cols] = result
-            lse_ref[p, b:b + 1, :] = logs
+            lse_ref[pair, b:b + 1, :] = logs
             for turn in range(pairs):
                 if (turn, b) in slots:
-                    @pl.when(p == turn)
+                    @pl.when(pair == turn)
                     def _():
                         for name, *units in slots[turn, b]:
                             run(name, *units)
@@ -405,17 +405,19 @@
 
     keep[3].start()
     keep[4].start()
-    run("arrive", o1, o2)
+    run("arrive", *n)
+    run("step3", *o)
+    run("arrive", *o)
     for copy in keep:
         copy.wait()
-    run("sent", vec, q1, q2, p1, p2, n1, n2, o1, o2)
+    run("sent", *units)
 
 
 def forward_part(tokens, seg_row, code_row, qkv, proj, inner, outer, rows16):
     rows, width = tokens.shape
     piece, ff = width // 32, inner.shape[1]
     pairs, blocks = width // (2 * HEAD), rows // BQ
-    at, wide_at = jnp.arange(width, dtype=jnp.int32)[None], jnp.arange(ff, dtype=jnp.int32)[None]
+    at, wide_at = np.arange(width, dtype=np.int32)[None], np.arange(ff, dtype=np.int32)[None]
     ins = (tokens, seg_row, code_row, at // piece, at % piece, wide_at // (ff // 32), wide_at % (ff // 32), qkv, proj, inner, outer, rows16)
     gathered = [jax.ShapeDtypeStruct((2, 2, 4, 2 * a.shape[0], a.shape[1]), a.dtype) for a in (qkv, proj, inner, outer)]
     made = [jax.ShapeDtypeStruct((width, rows), BF16), jax.ShapeDtypeStruct((3 * rows, width), BF16), jax.ShapeDtypeStruct((rows, width), BF16),
@@ -471,7 +473,7 @@
             copy.start()
 
     def add(self, target, other):
-        target[...] = (target[...].astype(F32) + other[...].astype(F32)).astype(target.dtype)
+        target[...] = target[...] + other[...]
 
     def step1(self):
         for copy in self.load:
@@ -479,34 +481,28 @@
         for copy in self.c0:
             copy.wait_recv()
 
-        @pl.loop(0, 16)
+        @pl.loop(0, 8)
         def _(j):
-            i = (j // 8, (j // 2) % 4, j % 2)
-            self.add(self.mine.at[i], self.r0.at[i])
+            self.add(self.mine.at[j // 4, j % 4], self.r0.at[j // 4, j % 4])
 
         self.c1.start()
 
     def step2(self):
         x, c, z, y = self.at
         self.c1.wait_recv()
-
-        @pl.loop(0, 8)
-        def _(j):
+        for i in range(4):
             if self.x_first:
-                self.add(self.mine.at[x, j // 2, j % 2], self.r1.at[j // 2, j % 2])
+                self.add(self.mine.at[x, i], self.r1.at[i])
             else:
-                self.add(self.mine.at[j // 4, j % 4, y], self.r1.at[j // 4, j % 4])
-
+                for j in range(2):
+                    self.add(self.mine.at[j, i, y], self.r1.at[j, i])
         self.c2.start()
 
     def step3(self):
         x, c, z, y = self.at
         self.c2.wait_recv()
-
-        @pl.loop(0, 4)
-        def _(j):
-            self.add(self.mine.at[x, j, y], self.r2.at[j])
-
+        for i in range(4):
+            self.add(self.mine.at[x, i, y], self.r2.at[i])
         for copy in self.z:
             copy.start()
 
@@ -575,9 +571,9 @@
     v_ref[...] = dv_acc[...].astype(BF16)
 
 
-B_UNITS = tuple((2, i * CHUNK, (i + 1) * CHUNK, i % 2 == 0) for i in range(6)) + (
+B_UNITS = tuple((2, i * CHUNK // 2, (i + 1) * CHUNK // 2, i % 2 == 0) for i in range(12)) + (
     (3, 0, 384, True), (3, 384, 768, False), (1, 0, 384, True), (1, 384, 768, False),
-    (0, 0, 1152, True), (0, 1152, 1792, False), (0, 1792, 2304, True), (4, 0, 128, True))
+    (0, 0, 640, True), (0, 640, 1152, False), (0, 1152, 1792, False), (0, 1792, 2304, True), (4, 0, 128, True))
 
 
 def backward_kernel(seg_ref, code_ref, piece_ref, lane_ref, wpiece_ref, wlane_ref, vecs_ref, ibias_ref, lse_ref, h2_hbm, cot_hbm,
@@ -608,7 +604,7 @@
     shares = (None, s_proj, s_inner, s_outer, s_vec)
     units = [Scatter(u, at, grads[k], slice(a, b), xf, bufs[5 * u:5 * u + 5], send, recv, local,
                      put_pairs(a, b) if k == 0 else put(shares[k], a, b)) for u, (k, a, b, xf) in enumerate(B_UNITS)]
-    n, o, p, (q1, q2, q3), v = units[:6], units[6:8], units[8:10], units[10:13], units[13]
+    n, o, p, q1, q2, v = [units[i:i + 2] for i in range(0, 12, 2)], units[12:14], units[14:16], units[16:18], units[18:20], units[20]
 
     tile = lambda ref, i, size: ref.at[:, pl.ds(pl.multiple_of(i * size, size), size)]
     band = lambda ref, i, size: ref.at[pl.ds(pl.multiple_of(i * size, size), size)]
@@ -679,7 +675,7 @@
             def _():
                 for name, lag in (("start", 1), ("step1", 2), ("step2", 3), ("step3", 4), ("finish", 5)):
                     if turn >= lag:
-                        run(name, n[turn - lag])
+                        run(name, *n[turn - lag])
 
     load_mixed.start()
     load_ht.start()
@@ -687,11 +683,11 @@
     load_wq.start()
     out_inner(chunks - 1).wait()
     out_outer(chunks - 1).wait()
-    run("start", n[5], *o)
-    run("step1", n[4])
-    run("step2", n[3])
-    run("step3", n[2])
-    run("finish", n[1])
+    run("start", *n[5], *o)
+    run("step1", *n[4])
+    run("step2", *n[3])
+    run("step3", *n[2])
+    run("finish", *n[1])
     load_resid.wait()
 
     @pl.loop(0, blocks)
@@ -712,23 +708,23 @@
 
     load_wp.wait()
     load_att.wait()
+    run("step1", *o)
 
     @pl.loop(0, rows // (2 * BQ))
     def _(rb):
         here = pl.ds(pl.multiple_of(rb * 2 * BQ, 2 * BQ), 2 * BQ)
         cot_ref[here, :] = nt(h2_ref[here, :], b_ref[:, 3 * width:]).astype(BF16)
 
-    run("step1", n[5])
-    run("step2", n[4])
-    run("step3", n[3])
-    run("finish", n[2])
+    run("step1", *n[5])
+    run("step2", *n[4])
+    run("step3", *n[3])
+    run("finish", *n[2])
     part = tn(att_ref[...], h2_ref[...]).astype(BF16)
     sto[0, :width // 2, :] = part[:width // 2]
     sto[1, :width // 2, :] = part[width // 2:]
     out_proj = [pltpu.make_async_copy(sto.at[i, :width // 2], band(g_proj, i, width // 2), stage.at[2 + i]) for i in range(2)]
     for copy in out_proj:
         copy.start()
-    run("step1", *o)
     load_mixed.wait()
     load_ht.wait()
     low_rows = lax.broadcasted_iota(jnp.int32, (2 * HEAD, BQ), 0) < HEAD
@@ -737,12 +733,12 @@
         copy.wait()
     run("start", *p)
     out_pair = lambda i: pltpu.make_async_copy(sti.at[i % 2, :, :3 * LANES], tile(g_qkv, i, 3 * LANES), stage.at[i % 2])
-    turns = {0: (("step2", n[5]), ("step3", n[4]), ("finish", n[3])),
-             1: (("step2", *o), ("step1", *p), ("step3", n[5]), ("finish", n[4])),
-             2: (("step2", *p), ("finish", n[5])),
-             3: (("start", q1), ("step3", *o)),
-             4: (("step1", q1), ("step3", *p), ("finish", *o)),
-             5: (("step2", q1), ("finish", *p))}
+    turns = {0: (("step2", *n[5]), ("step3", *n[4]), ("finish", *n[3]), ("step1", *p)),
+             1: (("step3", *n[5]), ("finish", *n[4])),
+             2: (("step2", *o), ("finish", *n[5])),
+             3: (("start", *q1), ("step2", *p)),
+             4: (("step1", *q1), ("step3", *o)),
+             5: (("step3", *p),)}
 
     @pl.loop(0, pairs)
     def _(i):
@@ -766,10 +762,9 @@
 
     load_tok.start()
     out_pair(pairs - 1).wait()
-    run("start", q2, q3)
+    run("start", *q2)
     load_wq.wait()
     load_tok.wait()
-    run("step3", q1)
 
     @pl.loop(0, rows // (2 * BQ))
     def _(rb):
@@ -780,11 +775,12 @@
             total = total + nt(a_ref[lines, :], b_ref[:, part * width:(part + 1) * width])
         acc2[here, :] = total
 
-        @pl.when(rb == 2)
+        @pl.when(rb == 0)
         def _():
-            run("step1", q2, q3)
-
-    run("step2", q2, q3)
+            run("step1", *q2)
+            run("step2", *q1)
+
+    run("step3", *q1)
 
     @pl.loop(0, blocks)
     def _(b):
@@ -793,6 +789,10 @@
         gtok_ref[here, :] = (acc1[here, :] + back).astype(BF16)
         sums[0:1, :] += gain
         sums[1:2, :] += shift
+
+        @pl.when(b == blocks // 2)
+        def _():
+            run("step2", *q2)
 
     pick, wide_pick = picker(lane_ref[...]), picker(wlane_ref[...])
     shard = lax.broadcasted_iota(jnp.int32, (32, width), 0)
@@ -805,13 +805,13 @@
     out_vec.start()
     out_vec.wait()
     run("start", v)
-    run("step3", q2, q3)
+    run("step3", *q2)
     run("step1", v)
-    run("finish", q1)
+    run("finish", *p, *o)
     run("step2", v)
-    run("finish", q2, q3)
+    run("finish", *q1)
     run("step3", v)
-    run("finish", v)
+    run("finish", *q2, v)
     run("sent", *units)
 
 
@@ -820,7 +820,7 @@
     ff = inner.shape[1]
     piece = width // 32
     blocks = rows // BQ
-    at, wide_at = jnp.arange(width, dtype=jnp.int32)[None], jnp.arange(ff, dtype=jnp.int32)[None]
+    at, wide_at = np.arange(width, dtype=np.int32)[None], np.arange(ff, dtype=np.int32)[None]
     fast = (seg_row, code_row, at // piece, at % piece, wide_at // (ff // 32), wide_at % (ff // 32), vecs, ibias, log_total)
     slow = (hidden_two, cotangent, tokens, resid, mixed, attended, h1t, qkv, proj, inner, outer)
     vmem, anywhere = pl.BlockSpec(memory_space=pltpu.VMEM), pl.BlockSpec(memory_space=pl.ANY)

time: 261 us -> 232 us (0.89)
  Pallas kernels: 244 us -> 216 us
    pallas_call x1, Pallas kernels: 149 us -> 128 us  [backward_part(): pl.pallas_call(backward_kernel, out_shape=[jax.ShapeDtypeStruct((rows, wi...]
    pallas_call x1, Pallas kernels: 94.6 us -> 87.5 us  [forward_part(): pl.pallas_call(forward_kernel, out_shape=gathered + made + small, in_spec...]
where the time goes in v1:
time: 232 us; the launch traced here: 231 us
  Pallas kernels  216 us (93%)
  local copies, waits for them, and re-layouts  12.8 us (6%)
    pallas_call x1, Pallas kernels, backward_part(): pl.pallas_call(backward_kernel, out_shape=[jax.ShapeDtypeStruct((rows, wi...  128 us
    pallas_call x1, Pallas kernels, forward_part(): pl.pallas_call(forward_kernel, out_shape=gathered + made + small, in_spec...  87.5 us
    unnamed x16, local copies, waits for them, and re-layouts  6.68 us

profile of v1, /device:TPU:0, one launch (start us, length us, event | category | flops | bytes accessed | tf_op | source)
XLA Modules:
  0.0 231.3 jit_solution(319190630593086952)
XLA Ops:
  0.6 0.7 pad_bitcast_fusion.8
  1.3 0.7 pad_bitcast_fusion.6
  2.0 0.7 pad_bitcast_fusion.4
  2.7 0.7 pad_bitcast_fusion.2
  3.3 0.7 pad_bitcast_fusion
  4.0 0.1 stack.49
  4.1 0.6 pad_convert_fusion.s_vec
  4.7 1.3 compare_select_fusion
  6.0 87.5 %forward_part.1 = (bf16[2,2,4,48,2304]{4,3,2,1,0:T(8,128)(2,1)}, bf16[2,2,4,48,768]{4,3,2,1,0:T(8,128)(2,1)}, bf16[2,2,4,48,3072]{4,3,2,1,0:T(8,128)(2,1)}, bf16...) custom-call(bf16[1024,768]{1,0:T(8,128)(2,1)} %tokens_hbm.1, ...), custom_call_target="tpu_custom_call" | custom-call | tf_op jit(solution)/shard_map/forward_part/pallas_call | solution.py:427
  93.4 128.4 %backward_part.1 = (bf16[1024,768]{1,0:T(8,128)(2,1)}, bf16[1024,768]{1,0:T(8,128)(2,1)}, f32[24,2304]{1,0:T(8,128)}, f32[24,768]{1,0:T(8,128)}, f32[24,3072]{1,...) custom-call(s32[1,1024]{1,0:T(1,128)} %bitcast.47, ...), custom_call_target="tpu_custom_call" | custom-call | tf_op jit(solution)/shard_map/backward_part/pallas_call | solution.py:835
  221.9 1.2 slice_bitcast_fusion.1
  223.1 1.5 slice_bitcast_fusion
  224.6 0.0 copy-start
  224.6 2.8 %copy.46 = bf16[1024,768]{1,0:T(8,128)(2,1)} copy(bf16[1024,768]{1,0:T(8,128)(2,1)} %get-tuple-element.84) | data formatting | bytes 3145728
  227.4 0.0 copy-done
  227.4 0.0 copy-start.3
  227.4 0.0 copy-start.4
  227.4 0.0 copy-start.2
  227.4 0.0 copy-start.1
  227.4 1.1 copy.47
  228.5 0.0 copy-done.3
  228.5 0.7 copy.48
  229.2 0.0 copy-done.4
  229.2 0.6 copy.49
  229.9 0.0 copy-done.2
  229.9 0.7 copy.50
  230.6 0.0 copy-done.1
  230.6 0.7 copy.51
Async XLA Ops:
  224.6 2.8 %copy-start = (bf16[1024,768]{1,0:T(8,128)(2,1)S(1)}, bf16[1024,768]{1,0:T(8,128)(2,1)}, u32[]{:S(2)}) copy-start(bf16[1024,768]{1,0:T(8,128)(2,1)} %get-tuple-element.85) | copy-start | bytes 4718596
  227.4 1.2 copy-start.3
  227.4 1.9 copy-start.4
  227.4 2.5 %copy-start.2 = (f32[24,3072]{1,0:T(8,128)S(1)}, f32[24,3072]{1,0:T(8,128)}, u32[]{:S(2)}) copy-start(f32[24,3072]{1,0:T(8,128)} %get-tuple-element.95) | copy-start | bytes 884740
  227.4 3.2 %copy-start.1 = (f32[96,768]{1,0:T(8,128)S(1)}, f32[96,768]{1,0:T(8,128)}, u32[]{:S(2)}) copy-start(f32[96,768]{1,0:T(8,128)} %get-tuple-element.97) | copy-start | bytes 884740
